TPU v7x, 32 devices: a whole 2x2x4 slice. The times are simulated.
32 devices in a mesh: row: 4 (over y, x), col: 8 (over z, core).
Axes of the slice: x: 2, y: 2, z: 4, core: 2. Of those that a mesh axis runs over, the one named last changes fastest.
Arguments:
- gains: float32 [512, 8, 256], P(('row', 'col')), may hold values from -6 to 6
- coherency: bfloat16 [512, 512, 8, 1, 256], P('row', 'col'), may hold values from -6 to 6
- cotangent: bfloat16 [512, 512, 8, 1, 8], P('row', 'col'), may hold values from -0.099609375 to 0.099609375
- flags: int32 [512, 512, 1], P('row', 'col'), may hold values 0 or 1
- station_slot: int32 [512], replicated, may hold values from 0 to 511, as said below
Outputs:
- gain_grad: float32 [512, 8, 256], P(('row', 'col'))
Inputs may be any that keep to these rules, and one draw needn't show every extreme that they name: `station_slot`: each station appears in exactly one slot; in every aligned block of 16 consecutive slots the stations lie with 16 different holders, station s being held by the device of index s // 16 in the order of row+col.
All inputs are finite; a program needn't handle non-finite values. No bound on the sum of `flags` on one device may be relied on, other than what follows from the above.
Results may differ from a plain program's by a relative error of at most 0.0003.
Values sent between devices are 32-bit elements; how exact they have to be, the bound alone decides.
A program may use at most 128 MiB of HBM per device.

v0:
```python
import jax
import jax.numpy as jnp
from jax import lax
from jax.sharding import PartitionSpec as P


def complex_product(first, second):
    return (
        first[0] * second[0] - first[1] * second[1],
        first[0] * second[1] + first[1] * second[0],
    )


def complex_sum(first, second):
    return (first[0] + second[0], first[1] + second[1])


def conjugate(element):
    return (element[0], -element[1])


def jones_product(first, second):
    return [
        complex_sum(
            complex_product(first[2 * row_index], second[column]),
            complex_product(first[2 * row_index + 1], second[2 + column]),
        )
        for row_index in (0, 1)
        for column in (0, 1)
    ]


def hermitian(matrix):
    return [conjugate(matrix[0]), conjugate(matrix[2]), conjugate(matrix[1]), conjugate(matrix[3])]


def as_complex(parts):
    return [(parts[0], parts[1]), (parts[2], parts[3]), (parts[4], parts[5]), (parts[6], parts[7])]


def as_parts(matrix):
    return [number for element in matrix for number in element]


def block_gradients(coherency, cotangent, flags, row_gains, col_gains):
    shape = coherency.shape
    directions = shape[4] // 8
    coherence = coherency.reshape(shape[:4] + (8, directions))
    weight = flags.astype(jnp.float32)[:, :, None, :, None]
    residual = as_complex(
        [
            cotangent[..., component].astype(jnp.float32)[..., None] * weight
            for component in range(8)
        ]
    )
    model_parts = as_complex(
        [coherence[..., component, :].astype(jnp.float32) for component in range(8)]
    )
    row_split = row_gains.reshape(row_gains.shape[0], row_gains.shape[1], 8, directions)
    col_split = col_gains.reshape(col_gains.shape[0], col_gains.shape[1], 8, directions)
    row_jones = as_complex([row_split[:, None, :, None, component, :] for component in range(8)])
    col_jones = as_complex([col_split[None, :, :, None, component, :] for component in range(8)])
    outgoing = jones_product(jones_product(residual, col_jones), hermitian(model_parts))
    row_side = jnp.stack([jnp.sum(part, axis=(1, 3)) for part in as_parts(outgoing)], axis=2)
    incoming = jones_product(jones_product(hermitian(residual), row_jones), model_parts)
    col_side = jnp.stack([jnp.sum(part, axis=(0, 3)) for part in as_parts(incoming)], axis=2)
    return (row_side.reshape(row_gains.shape), col_side.reshape(col_gains.shape))


def selector(identifiers, count):
    return (identifiers[:, None] == jnp.arange(count, dtype=jnp.int32)[None, :]).astype(jnp.float32)


def select_rows(table, values):
    return jnp.dot(
        table, values, precision=lax.Precision.HIGHEST, preferred_element_type=jnp.float32
    )


def shards(gains, coherency, cotangent, flags, station_slot):
    stations = station_slot.shape[0]
    share = gains.shape[0]
    flat = gains.shape[1] * gains.shape[2]
    row_total = lax.axis_size("row")
    col_total = lax.axis_size("col")
    groups = row_total * col_total
    row_place = lax.axis_index("row")
    col_place = lax.axis_index("col")
    device_place = row_place * col_total + col_place
    counting = jnp.arange(share, dtype=jnp.int32)
    slot_of = (
        jnp.zeros((stations,), jnp.int32)
        .at[station_slot]
        .set(jnp.arange(stations, dtype=jnp.int32))
    )
    own_blocks = jnp.take(slot_of, device_place * share + counting) // share
    col_target = own_blocks % row_total * col_total + own_blocks // row_total
    col_block = col_place * row_total + row_place
    row_holder = jnp.take(station_slot, device_place * share + counting) // share
    col_holder = jnp.take(station_slot, col_block * share + counting) // share
    row_count = coherency.shape[0]
    col_count = coherency.shape[1]
    row_ids = lax.dynamic_slice_in_dim(station_slot, row_place * row_count, row_count)
    col_ids = lax.dynamic_slice_in_dim(station_slot, col_place * col_count, col_count)
    every_gain = lax.all_gather(gains, ("row", "col"), axis=0, tiled=True)
    row_gains = jnp.take(every_gain, row_ids, axis=0)
    col_gains = jnp.take(every_gain, col_ids, axis=0)
    row_side, col_side = block_gradients(coherency, cotangent, flags, row_gains, col_gains)
    row_sum = lax.psum_scatter(row_side, "col", scatter_dimension=0, tiled=True)
    col_sum = lax.psum_scatter(col_side, "row", scatter_dimension=0, tiled=True)
    back_row = select_rows(selector(row_holder, groups).T, row_sum.reshape(share, flat))
    back_col = select_rows(selector(col_holder, groups).T, col_sum.reshape(share, flat))
    recv_row, recv_col = (
        lax.all_to_all(back_row, ("row", "col"), split_axis=0, concat_axis=0, tiled=True),
        lax.all_to_all(back_col, ("row", "col"), split_axis=0, concat_axis=0, tiled=True),
    )
    result = select_rows(selector(own_blocks, groups), recv_row) + select_rows(
        selector(col_target, groups), recv_col
    )
    return result.reshape(gains.shape)


def solution(mesh):
    placed = (
        P(("row", "col"), None, None),
        P("row", "col", None, None, None),
        P("row", "col", None, None, None),
        P("row", "col", None),
        P(),
    )
    return jax.shard_map(
        shards, mesh=mesh, in_specs=placed, out_specs=P(("row", "col"), None, None), check_vma=False
    )
```

profile of v0, /device:TPU:1, one launch (start us, length us, event | category | flops | bytes accessed | tf_op | source)
XLA Modules:
  0.0 435.6 jit_solution(9354245656156034932)
XLA Ops:
  8.1 47.1 %copy.64 = bf16[128,64,8,1,256]{0,4,2,1,3:T(8,128)(2,1)} copy(bf16[128,64,8,1,256]{4,2,3,1,0:T(8,128)(2,1)} %param.8) | data formatting | bytes 67108864 | tf_op args[1]
  55.4 3.4 fusion.96
  58.8 15.7 %all-gather.2.cloned.1.call-done = f32[512,8,256]{2,1,0:T(8,128)} async-done(((f32[16,8,256]{2,1,0:T(8,128)}), f32[512,8,256]{2,1,0:T(8,128)}) %all-gather.2.cloned.1.call-update) | async-done | bytes 4194320 | tf_op jit(solution)/shard_map/all_gather | solution.py:105
  74.5 2.8 gather_fusion
  79.2 23.2 %fusion.39 = f32[128,8,32]{0,2,1:T(8,128)} fusion(f32[128,64,8]{0,2,1:T(8,128)} %bitcast.345, f32[128,64,8]{0,2,1:T(8,128)S(1)} %bitcast.285, f32[128,64,8]{0,2,1:T(8,128)} %bitcast.341, f32[128,64,8]{0,2,1:T(8,128)S(1)} %bitcast.301, f32[64,8,32]{2,1,0:T(8,128)S(1)} %copy.70, f32[64,8,32]{2,1,0:T(8,128)S(1)} %copy.69, f32[64,8,32]{2,1,0:T(8,128)S(1)} %copy.68, ...), kind=kLoop, calls=%fused_computation.97 | loop fusion | flops 88047616 | bytes 18481152 | tf_op jit(solution)/shard_map/reduce_sum | solution.py:64
  102.4 23.1 %fusion.36 = f32[128,8,32]{0,2,1:T(8,128)} fusion(f32[128,64,8]{0,2,1:T(8,128)} %bitcast.346, f32[128,64,8]{0,2,1:T(8,128)S(1)} %bitcast.286, f32[128,64,8]{0,2,1:T(8,128)} %bitcast.342, f32[128,64,8]{0,2,1:T(8,128)S(1)} %bitcast.302, f32[64,8,32]{2,1,0:T(8,128)S(1)} %copy.70, f32[64,8,32]{2,1,0:T(8,128)S(1)} %copy.69, f32[64,8,32]{2,1,0:T(8,128)S(1)} %copy.68, ...), kind=kLoop, calls=%fused_computation.94 | loop fusion | flops 88047616 | bytes 18481152 | tf_op jit(solution)/shard_map/reduce_sum | solution.py:64
  125.5 18.5 %fusion.27 = f32[128,8,32]{0,2,1:T(8,128)S(1)} fusion(f32[128,64,8]{0,2,1:T(8,128)S(1)} %bitcast.347, f32[128,64,8]{0,2,1:T(8,128)S(1)} %bitcast.287, f32[128,64,8]{0,2,1:T(8,128)S(1)} %bitcast.343, f32[128,64,8]{0,2,1:T(8,128)S(1)} %bitcast.303, f32[64,8,32]{2,1,0:T(8,128)S(1)} %copy.70, f32[64,8,32]{2,1,0:T(8,128)S(1)} %copy.69, ...), kind=kLoop, calls=%fused_computation.85 | loop fusion | flops 88047616 | bytes 18481152 | tf_op jit(solution)/shard_map/reduce_sum | solution.py:64
  144.0 19.2 %fusion.24 = f32[128,8,32]{0,2,1:T(8,128)} fusion(f32[128,64,8]{0,2,1:T(8,128)S(1)} %bitcast.348, f32[128,64,8]{0,2,1:T(8,128)S(1)} %bitcast.288, f32[128,64,8]{0,2,1:T(8,128)S(1)} %bitcast.344, f32[128,64,8]{0,2,1:T(8,128)S(1)} %bitcast.304, f32[64,8,32]{2,1,0:T(8,128)S(1)} %copy.70, f32[64,8,32]{2,1,0:T(8,128)S(1)} %copy.69, f32[64,8,32]{2,1,0:T(8,128)S(1)} %copy.68, ...), kind=kLoop, calls=%fused_computation.82 | loop fusion | flops 88047616 | bytes 18481152 | tf_op jit(solution)/shard_map/reduce_sum | solution.py:64
  163.2 19.2 %fusion.33 = f32[128,8,32]{0,2,1:T(8,128)} fusion(f32[64,8,32]{2,1,0:T(8,128)S(1)} %copy.70, f32[64,8,32]{2,1,0:T(8,128)S(1)} %copy.69, f32[64,8,32]{2,1,0:T(8,128)S(1)} %copy.68, f32[64,8,32]{2,1,0:T(8,128)S(1)} %copy.67, f32[64,8,32]{2,1,0:T(8,128)S(1)} %copy.63, f32[128,64,8]{0,2,1:T(8,128)S(1)} %bitcast.337, f32[64,8,32]{2,1,0:T(8,128)S(1)} %copy.62, ...), kind=kLoop, calls=%fused_computation.91 | loop fusion | flops 88047616 | bytes 18481152 | tf_op jit(solution)/shard_map/reduce_sum | solution.py:64
  182.4 19.2 %fusion.18 = f32[128,8,32]{0,2,1:T(8,128)} fusion(f32[64,8,32]{2,1,0:T(8,128)S(1)} %copy.70, f32[64,8,32]{2,1,0:T(8,128)S(1)} %copy.69, f32[64,8,32]{2,1,0:T(8,128)S(1)} %copy.68, f32[64,8,32]{2,1,0:T(8,128)S(1)} %copy.67, f32[64,8,32]{2,1,0:T(8,128)S(1)} %copy.63, f32[128,64,8]{0,2,1:T(8,128)S(1)} %bitcast.338, f32[64,8,32]{2,1,0:T(8,128)S(1)} %copy.62, ...), kind=kLoop, calls=%fused_computation.76 | loop fusion | flops 88047616 | bytes 18481152 | tf_op jit(solution)/shard_map/reduce_sum | solution.py:64
  201.5 19.2 %fusion.30 = f32[128,8,32]{0,2,1:T(8,128)} fusion(f32[64,8,32]{2,1,0:T(8,128)S(1)} %copy.70, f32[64,8,32]{2,1,0:T(8,128)S(1)} %copy.69, f32[64,8,32]{2,1,0:T(8,128)S(1)} %copy.68, f32[64,8,32]{2,1,0:T(8,128)S(1)} %copy.67, f32[64,8,32]{2,1,0:T(8,128)S(1)} %copy.63, f32[128,64,8]{0,2,1:T(8,128)S(1)} %bitcast.339, f32[64,8,32]{2,1,0:T(8,128)S(1)} %copy.62, ...), kind=kLoop, calls=%fused_computation.88 | loop fusion | flops 88047616 | bytes 18481152 | tf_op jit(solution)/shard_map/reduce_sum | solution.py:64
  220.7 19.2 %fusion.21 = f32[128,8,32]{0,2,1:T(8,128)} fusion(f32[64,8,32]{2,1,0:T(8,128)S(1)} %copy.70, f32[64,8,32]{2,1,0:T(8,128)S(1)} %copy.69, f32[64,8,32]{2,1,0:T(8,128)S(1)} %copy.68, f32[64,8,32]{2,1,0:T(8,128)S(1)} %copy.67, f32[64,8,32]{2,1,0:T(8,128)S(1)} %copy.63, f32[128,64,8]{0,2,1:T(8,128)S(1)} %bitcast.340, f32[64,8,32]{2,1,0:T(8,128)S(1)} %copy.62, ...), kind=kLoop, calls=%fused_computation.79 | loop fusion | flops 88047616 | bytes 18481152 | tf_op jit(solution)/shard_map/reduce_sum | solution.py:64
  239.8 3.9 gather_fusion.1
  245.6 15.1 %fusion.69 = f32[64,8,32]{2,1,0:T(8,128)} fusion(f32[128,8,32]{0,2,1:T(8,128)S(1)} %get-tuple-element.31, f32[128,8,32]{0,2,1:T(8,128)S(1)} %get-tuple-element.32, f32[128,8,32]{0,2,1:T(8,128)S(1)} %get-tuple-element.33, f32[128,8,32]{0,2,1:T(8,128)S(1)} %get-tuple-element.34, f32[128,8,32]{0,2,1:T(8,128)S(1)} %get-tuple-element.35, ...), kind=kLoop, calls=%fused_computation.127 | loop fusion | flops 83869696 | bytes 18939904 | tf_op jit(solution)/shard_map/reduce_sum | solution.py:66
  260.7 14.7 %fusion.66 = f32[64,8,32]{2,1,0:T(8,128)} fusion(f32[128,8,32]{0,2,1:T(8,128)S(1)} %get-tuple-element.31, f32[128,8,32]{0,2,1:T(8,128)S(1)} %get-tuple-element.32, f32[128,8,32]{0,2,1:T(8,128)S(1)} %get-tuple-element.33, f32[128,8,32]{0,2,1:T(8,128)S(1)} %get-tuple-element.34, f32[128,8,32]{0,2,1:T(8,128)S(1)} %get-tuple-element.35, ...), kind=kLoop, calls=%fused_computation.124 | loop fusion | flops 83869696 | bytes 18939904 | tf_op jit(solution)/shard_map/reduce_sum | solution.py:66
  275.4 14.7 %fusion.53 = f32[64,8,32]{2,1,0:T(8,128)} fusion(f32[128,8,32]{0,2,1:T(8,128)S(1)} %get-tuple-element.31, f32[128,8,32]{0,2,1:T(8,128)S(1)} %get-tuple-element.32, f32[128,8,32]{0,2,1:T(8,128)S(1)} %get-tuple-element.33, f32[128,8,32]{0,2,1:T(8,128)S(1)} %get-tuple-element.34, f32[128,8,32]{0,2,1:T(8,128)S(1)} %get-tuple-element.35, ...), kind=kLoop, calls=%fused_computation.111 | loop fusion | flops 83869696 | bytes 18939904 | tf_op jit(solution)/shard_map/reduce_sum | solution.py:66
  290.2 12.3 %fusion.50 = f32[64,8,32]{2,1,0:T(8,128)} fusion(f32[128,8,32]{0,2,1:T(8,128)S(1)} %get-tuple-element.31, f32[128,8,32]{0,2,1:T(8,128)S(1)} %get-tuple-element.32, f32[128,8,32]{0,2,1:T(8,128)S(1)} %get-tuple-element.33, f32[128,8,32]{0,2,1:T(8,128)S(1)} %get-tuple-element.34, f32[128,8,32]{0,2,1:T(8,128)S(1)} %get-tuple-element.35, ...), kind=kLoop, calls=%fused_computation.108 | loop fusion | flops 83869696 | bytes 18939904 | tf_op jit(solution)/shard_map/reduce_sum | solution.py:66
  302.5 12.5 %fusion.56 = f32[64,8,32]{2,1,0:T(8,128)} fusion(f32[128,64,8]{0,2,1:T(8,128)S(1)} %bitcast.317, f32[128,64,8]{0,2,1:T(8,128)S(1)} %bitcast.321, f32[128,8,32]{0,2,1:T(8,128)S(1)} %get-tuple-element.31, f32[128,8,32]{0,2,1:T(8,128)S(1)} %get-tuple-element.32, f32[128,8,32]{0,2,1:T(8,128)S(1)} %get-tuple-element.33, f32[128,8,32]{0,2,1:T(8,128)S(1)} %get-tuple-element.34, ...), kind=kLoop, calls=%fused_computation.114 | loop fusion | flops 83869696 | bytes 18939904 | tf_op jit(solution)/shard_map/reduce_sum | solution.py:66
  315.0 11.6 %fusion.72 = f32[64,8,32]{2,1,0:T(8,128)S(1)} fusion(f32[128,64,8]{0,2,1:T(8,128)S(1)} %bitcast.318, f32[128,64,8]{0,2,1:T(8,128)S(1)} %bitcast.322, f32[128,8,32]{0,2,1:T(8,128)S(1)} %get-tuple-element.31, f32[128,8,32]{0,2,1:T(8,128)S(1)} %get-tuple-element.32, f32[128,8,32]{0,2,1:T(8,128)S(1)} %get-tuple-element.33, ...), kind=kLoop, calls=%fused_computation.130 | loop fusion | flops 83869696 | bytes 18939904 | tf_op jit(solution)/shard_map/reduce_sum | solution.py:66
  326.6 11.6 %fusion.59 = f32[64,8,32]{2,1,0:T(8,128)S(1)} fusion(f32[128,64,8]{0,2,1:T(8,128)S(1)} %bitcast.319, f32[128,64,8]{0,2,1:T(8,128)S(1)} %bitcast.323, f32[128,8,32]{0,2,1:T(8,128)S(1)} %get-tuple-element.31, f32[128,8,32]{0,2,1:T(8,128)S(1)} %get-tuple-element.32, f32[128,8,32]{0,2,1:T(8,128)S(1)} %get-tuple-element.33, ...), kind=kLoop, calls=%fused_computation.117 | loop fusion | flops 83869696 | bytes 18939904 | tf_op jit(solution)/shard_map/reduce_sum | solution.py:66
  347.6 1.6 bitcast_dynamic-update-slice_fusion.9
  349.9 2.6 copy.76
  352.6 1.7 bitcast_dynamic-update-slice_fusion.7
  354.3 1.7 bitcast_dynamic-update-slice_fusion.6
  357.4 1.7 bitcast_dynamic-update-slice_fusion.3
  360.5 13.9 %fusion.75 = f32[64,8,32]{2,1,0:T(8,128)S(1)} fusion(f32[128,64,8]{0,2,1:T(8,128)S(1)} %bitcast.320, f32[128,64,8]{0,2,1:T(8,128)S(1)} %bitcast.324, f32[128,8,32]{0,2,1:T(8,128)S(1)} %get-tuple-element.31, f32[128,8,32]{0,2,1:T(8,128)S(1)} %get-tuple-element.32, f32[128,8,32]{0,2,1:T(8,128)S(1)} %get-tuple-element.33, ...), kind=kLoop, calls=%fused_computation.133 | loop fusion | flops 83869696 | bytes 18939904 | tf_op jit(solution)/shard_map/reduce_sum | solution.py:66
  375.1 2.2 copy.79
  382.5 6.6 %all-to-all-start = ((f32[32,1,2048]{2,1,0:T(1,128)}), f32[32,1,2048]{2,1,0:T(1,128)S(1)}, u32[]{:S(2)}, u32[]{:S(2)}) async-start(f32[32,1,2048]{2,1,0:T(1,128)} %copy.77), calls=%async_computation.1 | async-start | bytes 524288 | tf_op jit(solution)/shard_map/all_to_all | solution.py:114
  389.8 20.0 %reduce-scatter.5.cloned.1.call-done = f32[16,8,256]{2,1,0:T(8,128)} async-done(((f32[64,8,256]{2,1,0:T(8,128)}), f32[16,8,256]{2,1,0:T(8,128)}) %reduce-scatter.5.cloned.1.call-update) | async-done | bytes 131088 | tf_op jit(solution)/shard_map/reduce_scatter | solution.py:110
  412.1 5.4 %all-to-all-start.1 = ((f32[32,1,2048]{2,1,0:T(1,128)}), f32[32,1,2048]{2,1,0:T(1,128)S(1)}, u32[]{:S(2)}, u32[]{:S(2)}) async-start(f32[32,1,2048]{2,1,0:T(1,128)} %copy.81), calls=%async_computation.3 | async-start | bytes 524288 | tf_op jit(solution)/shard_map/all_to_all | solution.py:115
  417.6 2.4 scatter_custom_fusion
  421.0 7.0 %all-to-all-done.1 = f32[32,1,2048]{2,1,0:T(1,128)S(1)} async-done(((f32[32,1,2048]{2,1,0:T(1,128)}), f32[32,1,2048]{2,1,0:T(1,128)S(1)}, u32[]{:S(2)}, u32[]{:S(2)}) %all-to-all-start.1) | async-done | bytes 262176 | tf_op jit(solution)/shard_map/all_to_all | solution.py:115
  (102 shorter events, 29.3 us)
Async XLA Ops:
  6.5 68.0 %all-gather.2.cloned.1.call-start = ((), (), s32[]{:S(2)}) async-start(), calls=%async_computation.4 | async-start | bytes 4325376 | tf_op jit(solution)/shard_map/all_gather | solution.py:105
  7.3 373.0 %reduce-scatter.3.cloned.1.call-start = ((), (), s32[]{:S(2)}) async-start(), calls=%async_computation.5 | async-start | bytes 1179648 | tf_op jit(solution)/shard_map/reduce_scatter | solution.py:109
  8.1 47.1 %copy-start.1 = (s32[512]{0:T(512)S(1)}, s32[512]{0:T(512)}, u32[]{:S(2)}) copy-start(s32[512]{0:T(512)} %param.11) | copy-start | bytes 6148
  8.1 47.3 %copy-start.10 = (bf16[128,64,8,1,8]{0,4,3,2,1:T(8,128)(2,1)S(1)}, bf16[128,64,8,1,8]{0,4,3,2,1:T(8,128)(2,1)}, u32[]{:S(2)}) copy-start(bf16[128,64,8,1,8]{0,4,3,2,1:T(8,128)(2,1)} %param.9) | copy-start | bytes 3145732
  79.2 46.3 %copy-start = (bf16[128,64,8,1,256]{0,4,2,1,3:T(8,128)(2,1)S(1)}, bf16[128,64,8,1,256]{0,4,2,1,3:T(8,128)(2,1)}, u32[]{:S(2)}) copy-start(bf16[128,64,8,1,256]{0,4,2,1,3:T(8,128)(2,1)} %copy.64) | copy-start | bytes 100663296
  102.4 23.1 %copy-start.8 = (f32[128,64,8,1,1]{0,4,3,2,1:T(1,128)S(1)}, f32[128,64,8,1,1]{0,4,3,2,1:T(1,128)}, u32[]{:S(2)}) copy-start(f32[128,64,8,1,1]{0,4,3,2,1:T(1,128)} %get-tuple-element.15) | copy-start | bytes 786436
  102.4 23.1 %copy-start.9 = (f32[128,64,8,1,1]{0,4,3,2,1:T(1,128)S(1)}, f32[128,64,8,1,1]{0,4,3,2,1:T(1,128)}, u32[]{:S(2)}) copy-start(f32[128,64,8,1,1]{0,4,3,2,1:T(1,128)} %get-tuple-element.25) | copy-start | bytes 786436
  144.0 19.2 %copy-start.6 = (f32[128,64,8,1,1]{0,4,3,2,1:T(1,128)S(1)}, f32[128,64,8,1,1]{0,4,3,2,1:T(1,128)}, u32[]{:S(2)}) copy-start(f32[128,64,8,1,1]{0,4,3,2,1:T(1,128)} %get-tuple-element.22) | copy-start | bytes 786436
  144.0 19.2 %copy-start.7 = (f32[128,64,8,1,1]{0,4,3,2,1:T(1,128)S(1)}, f32[128,64,8,1,1]{0,4,3,2,1:T(1,128)}, u32[]{:S(2)}) copy-start(f32[128,64,8,1,1]{0,4,3,2,1:T(1,128)} %get-tuple-element.29) | copy-start | bytes 786436
  239.8 5.7 %copy-start.4 = (f32[128,64,8,1,1]{0,4,3,2,1:T(1,128)S(1)}, f32[128,64,8,1,1]{0,4,3,2,1:T(1,128)}, u32[]{:S(2)}) copy-start(f32[128,64,8,1,1]{0,4,3,2,1:T(1,128)} %get-tuple-element.14) | copy-start | bytes 786436
  239.8 5.7 %copy-start.5 = (f32[128,64,8,1,1]{0,4,3,2,1:T(1,128)S(1)}, f32[128,64,8,1,1]{0,4,3,2,1:T(1,128)}, u32[]{:S(2)}) copy-start(f32[128,64,8,1,1]{0,4,3,2,1:T(1,128)} %get-tuple-element.21) | copy-start | bytes 786436
  245.3 44.9 %slice-start = ((s8[33554432]{0:T(1024)(128)(4,1)}), s8[4194304]{0:T(1024)(128)(4,1)S(1)}, s32[]{:S(2)}) async-start(s8[33554432]{0:T(1024)(128)(4,1)} %bitcast.279), calls=%async_computation.7 | async-start | bytes 8388608
  245.5 44.6 %slice-start.1 = ((s8[33554432]{0:T(1024)(128)(4,1)}), s8[4194304]{0:T(1024)(128)(4,1)S(1)}, s32[]{:S(2)}) async-start(s8[33554432]{0:T(1024)(128)(4,1)} %bitcast.279), calls=%async_computation.8 | async-start | bytes 8388608
  245.5 44.6 %slice-start.2 = ((s8[33554432]{0:T(1024)(128)(4,1)}), s8[4194304]{0:T(1024)(128)(4,1)S(1)}, s32[]{:S(2)}) async-start(s8[33554432]{0:T(1024)(128)(4,1)} %bitcast.279), calls=%async_computation.9 | async-start | bytes 8388608
  245.6 44.6 %slice-start.3 = ((s8[33554432]{0:T(1024)(128)(4,1)}), s8[4194304]{0:T(1024)(128)(4,1)S(1)}, s32[]{:S(2)}) async-start(s8[33554432]{0:T(1024)(128)(4,1)} %bitcast.279), calls=%async_computation.10 | async-start | bytes 8388608
  260.7 29.5 %slice-start.4 = ((s8[33554432]{0:T(1024)(128)(4,1)}), s8[4194304]{0:T(1024)(128)(4,1)S(1)}, s32[]{:S(2)}) async-start(s8[33554432]{0:T(1024)(128)(4,1)} %bitcast.279), calls=%async_computation.11 | async-start | bytes 8388608
  260.7 29.5 %slice-start.5 = ((s8[33554432]{0:T(1024)(128)(4,1)}), s8[4194304]{0:T(1024)(128)(4,1)S(1)}, s32[]{:S(2)}) async-start(s8[33554432]{0:T(1024)(128)(4,1)} %bitcast.279), calls=%async_computation.12 | async-start | bytes 8388608
  275.4 14.8 %slice-start.6 = ((s8[33554432]{0:T(1024)(128)(4,1)}), s8[4194304]{0:T(1024)(128)(4,1)S(1)}, s32[]{:S(2)}) async-start(s8[33554432]{0:T(1024)(128)(4,1)} %bitcast.279), calls=%async_computation.13 | async-start | bytes 8388608
  275.4 14.8 %slice-start.7 = ((s8[33554432]{0:T(1024)(128)(4,1)}), s8[4194304]{0:T(1024)(128)(4,1)S(1)}, s32[]{:S(2)}) async-start(s8[33554432]{0:T(1024)(128)(4,1)} %bitcast.279), calls=%async_computation.14 | async-start | bytes 8388608
  290.2 12.3 %copy-start.2 = (f32[128,64,8,1,1]{0,4,3,2,1:T(1,128)S(1)}, f32[128,64,8,1,1]{0,4,3,2,1:T(1,128)}, u32[]{:S(2)}) copy-start(f32[128,64,8,1,1]{0,4,3,2,1:T(1,128)} %get-tuple-element.24) | copy-start | bytes 786436
  290.2 12.3 %copy-start.3 = (f32[128,64,8,1,1]{0,4,3,2,1:T(1,128)S(1)}, f32[128,64,8,1,1]{0,4,3,2,1:T(1,128)}, u32[]{:S(2)}) copy-start(f32[128,64,8,1,1]{0,4,3,2,1:T(1,128)} %get-tuple-element.28) | copy-start | bytes 786436
  326.6 29.3 %copy-start.12 = (f32[64,8,32]{2,1,0:T(8,128)S(1)}, f32[64,8,32]{2,1,0:T(8,128)}, u32[]{:S(2)}) copy-start(f32[64,8,32]{2,1,0:T(8,128)} %fusion.66) | copy-start | bytes 196612
  326.6 30.0 %copy-start.11 = (f32[64,8,32]{2,1,0:T(8,128)S(1)}, f32[64,8,32]{2,1,0:T(8,128)}, u32[]{:S(2)}) copy-start(f32[64,8,32]{2,1,0:T(8,128)} %fusion.69) | copy-start | bytes 196612
  352.5 57.3 %reduce-scatter.5.cloned.1.call-start = ((), (), s32[]{:S(2)}) async-start(), calls=%async_computation.6 | async-start | bytes 655360 | tf_op jit(solution)/shard_map/reduce_scatter | solution.py:110
  382.5 29.6 %all-to-all-start = ((f32[32,1,2048]{2,1,0:T(1,128)}), f32[32,1,2048]{2,1,0:T(1,128)S(1)}, u32[]{:S(2)}, u32[]{:S(2)}) async-start(f32[32,1,2048]{2,1,0:T(1,128)} %copy.77), calls=%async_computation.1 | async-start | bytes 524288 | tf_op jit(solution)/shard_map/all_to_all | solution.py:114
  412.1 15.9 %all-to-all-start.1 = ((f32[32,1,2048]{2,1,0:T(1,128)}), f32[32,1,2048]{2,1,0:T(1,128)S(1)}, u32[]{:S(2)}, u32[]{:S(2)}) async-start(f32[32,1,2048]{2,1,0:T(1,128)} %copy.81), calls=%async_computation.3 | async-start | bytes 524288 | tf_op jit(solution)/shard_map/all_to_all | solution.py:115
Sparse Core Ops, SparseCore 0:
  10.3 64.1 all-gather.1
  352.7 27.5 reduce-scatter.2
  383.0 26.7 reduce-scatter.4
where the time goes:
time: 437 us; the launch traced here: 436 us
  other arithmetic  272 us (62%)
  local copies, waits for them, and re-layouts  92.4 us (21%)
  waiting for transfers between devices  44.5 us (10%)
  between operations  13.6 us (3%)
  starting transfers between devices  12.1 us (3%)
    reduce_sum x8, other arithmetic, block_gradients(): jnp.sum(part, axis=(1, 3))  161 us
    reduce_sum x8, other arithmetic, block_gradients(): jnp.sum(part, axis=(0, 3))  106 us
    unnamed x60, local copies, waits for them, and re-layouts  68.7 us
    reduce_scatter x1, waiting for transfers between devices, shards(): col_sum = lax.psum_scatter(col_side, 'row', scatter_dimension=0, tiled=True)  20 us
    all_gather x1, waiting for transfers between devices, shards(): every_gain = lax.all_gather(gains, ('row', 'col'), axis=0, tiled=True)  15.7 us
  transfers between devices with their start and end apart: 5, of which 4 were waited for; matrix products, arithmetic and copies ran while one was open for 20% of the time, Pallas kernels for 0%

commit v1 on v0

v1 whole, which is shorter than its diff:
```python
import functools

import jax
import jax.numpy as jnp
from jax import lax
from jax.experimental import pallas as pl
from jax.experimental.pallas import tpu as pltpu
from jax.sharding import PartitionSpec as P


def swap_pairs(values, width, even):
    return jnp.where(even, pltpu.roll(values, 3 * width, 1), pltpu.roll(values, width, 1))


def two_parts(values):
    high = values.astype(jnp.bfloat16)
    return high, (values - high.astype(jnp.float32)).astype(jnp.bfloat16)


def row_weights(gains, width, even, sign):
    lanes = 4 * width
    rows = []
    for b in range(2):
        half = gains[:, b * lanes : (b + 1) * lanes]
        rows += [half, -sign * swap_pairs(half, width, even)]
    tables = []
    for part in two_parts(jnp.concatenate(rows, axis=0)):
        zero = jnp.zeros_like(part)
        tables += [
            jnp.concatenate([part, zero], axis=1),
            jnp.concatenate([zero, part], axis=1),
        ]
    return jnp.concatenate(tables, axis=0)


def col_weights(gains, width, even, sign, group):
    lanes = 4 * width
    blocks = []
    for b in range(2):
        half = gains[:, b * lanes : (b + 1) * lanes]
        other = pltpu.roll(half, 2 * width, 1)
        rows = [[], []]
        for e in range(2):
            twice = jnp.where(group // 2 == e, half, other)
            rows[0].append(sign * twice)
            rows[1].append(swap_pairs(twice, width, even))
        blocks.append(
            jnp.concatenate([jnp.concatenate(row, axis=1) for row in rows], axis=0)
        )
    tables = []
    for part in range(2):
        for b in range(2):
            value = two_parts(blocks[b])[part]
            zero = jnp.zeros_like(value)
            tables += [
                jnp.concatenate([value, zero], axis=1),
                jnp.concatenate([zero, value], axis=1),
            ]
    return jnp.concatenate(tables, axis=0)


def gradient_kernel(
    width, m_ref, g_ref, gt_ref, jr_ref, jc_ref, r_ref, c_ref,
    wr_ref, wc_ref, xr_ref, xa_ref, xb_ref, acc_ref,
):
    block, second, channels, _ = m_ref.shape
    lanes = 4 * width
    depth = g_ref.shape[2]
    pair = xa_ref.shape[0]
    chunk = xa_ref.shape[1] // channels
    chunks = second // chunk
    step = pl.program_id(0)

    lane_f = lax.broadcasted_iota(jnp.int32, (channels, depth), 1) % channels
    sub_f = lax.broadcasted_iota(jnp.int32, (channels, depth), 0)
    diagonal = (lane_f == sub_f).astype(jnp.float32)
    group = lax.broadcasted_iota(jnp.int32, (channels, lanes), 1) // width
    even = group % 2 == 0
    sign = jnp.where(even, 1.0, -1.0)

    @pl.when(step == 0)
    def _():
        acc_ref[...] = jnp.zeros_like(acc_ref)

        def prepare(k, carry):
            wr_ref[k] = row_weights(jc_ref[k], width, even, sign)
            return carry

        lax.fori_loop(0, second, prepare, 0)

    def spread(rows):
        count = rows.shape[0]
        wide = rows[:, None, :] * diagonal[None]
        return wide.reshape(count * channels, depth).astype(jnp.bfloat16)

    def row_products(k, carry):
        xr_ref[k] = jnp.dot(
            spread(gt_ref[k]), wr_ref[k], preferred_element_type=jnp.float32
        )
        return carry

    lax.fori_loop(0, second, row_products, 0, unroll=4)

    def stations(pair_index, carry):
        first = pair_index * pair
        for p in range(pair):
            wc_ref[p] = col_weights(jr_ref[first + p], width, even, sign, group)

        def col_products(at, x_ref):
            start = pl.multiple_of(at * chunk, chunk)
            for p in range(pair):
                x_ref[p] = jnp.dot(
                    spread(g_ref[first + p, pl.ds(start, chunk)]),
                    wc_ref[p],
                    preferred_element_type=jnp.float32,
                )

        def combine(at, x_ref, totals):
            totals = list(totals)
            for q in range(chunk):
                k = at * chunk + q
                col = [acc_ref[k, n] for n in range(4)]
                for p in range(pair):
                    m = m_ref[first + p, k].astype(jnp.float32)
                    halves = [m[:, :lanes], m[:, lanes:]]
                    swapped = [swap_pairs(h, width, even) for h in halves]
                    start = pl.multiple_of((first + p) * channels, channels)
                    for a in range(2):
                        x = xr_ref[k, pl.ds(start, channels), a * lanes : (a + 1) * lanes]
                        for c in range(2):
                            n = p * 8 + 4 * a + 2 * c
                            totals[n] = totals[n] + x * halves[c]
                            totals[n + 1] = totals[n + 1] + x * swapped[c]
                    for a in range(2):
                        for e in range(2):
                            n = 2 * a + e
                            y = x_ref[
                                p,
                                q * channels : (q + 1) * channels,
                                n * lanes : (n + 1) * lanes,
                            ]
                            col[2 * a] = col[2 * a] + y * halves[e]
                            col[2 * a + 1] = col[2 * a + 1] + y * swapped[e]
                for n in range(4):
                    acc_ref[k, n] = col[n]
            return tuple(totals)

        def two_chunks(j, totals):
            col_products(2 * j + 1, xb_ref)
            totals = combine(2 * j, xa_ref, totals)
            col_products(jnp.minimum(2 * j + 2, chunks - 1), xa_ref)
            return combine(2 * j + 1, xb_ref, totals)

        zero = jnp.zeros((channels, lanes), jnp.float32)
        col_products(0, xa_ref)
        totals = lax.fori_loop(0, chunks // 2, two_chunks, (zero,) * (8 * pair))
        for p in range(pair):
            for a in range(2):
                parts = []
                for n in range(4):
                    value = totals[8 * p + 4 * a + n]
                    if n % 2 == 1:
                        value = -sign * value
                    value = value + pltpu.roll(value, 2 * width, 1)
                    parts.append(value + pltpu.roll(value, width, 1))
                r_ref[first + p, :, a * lanes : (a + 1) * lanes] = jnp.where(
                    group < 2,
                    jnp.where(even, parts[0], parts[1]),
                    jnp.where(even, parts[2], parts[3]),
                )
        return carry

    lax.fori_loop(0, block // pair, stations, 0)

    @pl.when(step == pl.num_programs(0) - 1)
    def _():
        def finish(k, carry):
            for a in range(2):
                real = acc_ref[k, 2 * a]
                imag = acc_ref[k, 2 * a + 1] * sign
                real = real + swap_pairs(real, width, even)
                imag = imag + swap_pairs(imag, width, even)
                c_ref[k, :, a * lanes : (a + 1) * lanes] = jnp.where(even, real, imag)
            return carry

        lax.fori_loop(0, second, finish, 0, unroll=2)


def residuals(cotangent, flags):
    first, second, channels = cotangent.shape[:3]
    weighted = cotangent[:, :, :, 0].astype(jnp.float32) * flags.astype(jnp.float32)[..., None]
    lane_order = weighted.transpose(0, 1, 3, 2).reshape(first, second, 8 * channels)
    doubled = jnp.concatenate([lane_order, lane_order], axis=-1)
    return doubled, doubled.transpose(1, 0, 2)


def block_gradients(coherency, doubled, across, row_gains, col_gains):
    first, second, channels, _, wide = coherency.shape
    width = wide // 8
    block = min(16, first)
    pair = 2
    chunk = min(16, second // 2)
    depth = doubled.shape[2]
    model = coherency.reshape(first, second, channels, wide)
    products = (pair, chunk * channels, 2 * wide)
    return pl.pallas_call(
        functools.partial(gradient_kernel, width),
        grid=(first // block,),
        in_specs=[
            pl.BlockSpec((block, second, channels, wide), lambda s: (s, 0, 0, 0)),
            pl.BlockSpec((block, second, depth), lambda s: (s, 0, 0)),
            pl.BlockSpec((second, block, depth), lambda s: (0, s, 0)),
            pl.BlockSpec((block, channels, wide), lambda s: (s, 0, 0)),
            pl.BlockSpec((second, channels, wide), lambda s: (0, 0, 0)),
        ],
        out_specs=[
            pl.BlockSpec((block, channels, wide), lambda s: (s, 0, 0)),
            pl.BlockSpec((second, channels, wide), lambda s: (0, 0, 0)),
        ],
        out_shape=[
            jax.ShapeDtypeStruct((first, channels, wide), jnp.float32),
            jax.ShapeDtypeStruct((second, channels, wide), jnp.float32),
        ],
        scratch_shapes=[
            pltpu.VMEM((second, depth, wide), jnp.bfloat16),
            pltpu.VMEM((pair, depth, 2 * wide), jnp.bfloat16),
            pltpu.VMEM((second, block * channels, wide), jnp.float32),
            pltpu.VMEM(products, jnp.float32),
            pltpu.VMEM(products, jnp.float32),
            pltpu.VMEM((second, 4, channels, wide // 2), jnp.float32),
        ],
        compiler_params=pltpu.CompilerParams(
            dimension_semantics=("arbitrary",), vmem_limit_bytes=58 * 1024 * 1024
        ),
    )(model, doubled, across, row_gains, col_gains)


def selector(identifiers, count):
    return (identifiers[:, None] == jnp.arange(count, dtype=jnp.int32)[None, :]).astype(jnp.float32)


def select_rows(table, values):
    return jnp.dot(
        table, values, precision=lax.Precision.HIGHEST, preferred_element_type=jnp.float32
    )


def shards(gains, coherency, cotangent, flags, station_slot):
    stations = station_slot.shape[0]
    share = gains.shape[0]
    flat = gains.shape[1] * gains.shape[2]
    row_total = lax.axis_size("row")
    col_total = lax.axis_size("col")
    groups = row_total * col_total
    row_place = lax.axis_index("row")
    col_place = lax.axis_index("col")
    device_place = row_place * col_total + col_place
    counting = jnp.arange(share, dtype=jnp.int32)
    slot_of = (
        jnp.zeros((stations,), jnp.int32)
        .at[station_slot]
        .set(jnp.arange(stations, dtype=jnp.int32))
    )
    own_blocks = jnp.take(slot_of, device_place * share + counting) // share
    col_target = own_blocks % row_total * col_total + own_blocks // row_total
    col_block = col_place * row_total + row_place
    row_holder = jnp.take(station_slot, device_place * share + counting) // share
    col_holder = jnp.take(station_slot, col_block * share + counting) // share
    row_count = coherency.shape[0]
    col_count = coherency.shape[1]
    row_ids = lax.dynamic_slice_in_dim(station_slot, row_place * row_count, row_count)
    col_ids = lax.dynamic_slice_in_dim(station_slot, col_place * col_count, col_count)
    every_gain = lax.all_gather(gains, ("row", "col"), axis=0, tiled=True)
    row_gains = jnp.take(every_gain, row_ids, axis=0)
    col_gains = jnp.take(every_gain, col_ids, axis=0)
    row_side, col_side = block_gradients(
        coherency, *residuals(cotangent, flags), row_gains, col_gains
    )
    row_sum = lax.psum_scatter(row_side, "col", scatter_dimension=0, tiled=True)
    col_sum = lax.psum_scatter(col_side, "row", scatter_dimension=0, tiled=True)
    back_row = select_rows(selector(row_holder, groups).T, row_sum.reshape(share, flat))
    back_col = select_rows(selector(col_holder, groups).T, col_sum.reshape(share, flat))
    recv_row, recv_col = (
        lax.all_to_all(back_row, ("row", "col"), split_axis=0, concat_axis=0, tiled=True),
        lax.all_to_all(back_col, ("row", "col"), split_axis=0, concat_axis=0, tiled=True),
    )
    result = select_rows(selector(own_blocks, groups), recv_row) + select_rows(
        selector(col_target, groups), recv_col
    )
    return result.reshape(gains.shape)


def solution(mesh):
    placed = (
        P(("row", "col"), None, None),
        P("row", "col", None, None, None),
        P("row", "col", None, None, None),
        P("row", "col", None),
        P(),
    )
    return jax.shard_map(
        shards, mesh=mesh, in_specs=placed, out_specs=P(("row", "col"), None, None), check_vma=False
    )
```

time: 437 us -> 303 us (0.69)
  other arithmetic: 272 us -> 11.3 us
  Pallas kernels: 0 us -> 137 us
  local copies, waits for them, and re-layouts: 92.4 us -> 21.7 us
  waiting for transfers between devices: 44.5 us -> 106 us
    reduce_sum x16 -> x0, other arithmetic: 267 us -> none  [the longest x8 161 us: block_gradients(): jnp.sum(part, axis=(1, 3))]
    pallas_call x0 -> x1, Pallas kernels: none -> 137 us  [block_gradients(): pl.pallas_call(functools.partial(gradient_kernel, width), grid=(first //...]
    unnamed x60 -> x5, local copies, waits for them, and re-layouts: 68.7 us -> 2.59 us
    all_gather x1, waiting for transfers between devices: 15.7 us -> 51 us  [shards(): every_gain = lax.all_gather(gains, ('row', 'col'), axis=0, tiled=True)]
    reduce_scatter x1, waiting for transfers between devices: 1.02 us -> 26.3 us  [shards(): row_sum = lax.psum_scatter(row_side, 'col', scatter_dimension=0, tiled=True)]
    transpose x0 -> x1, other arithmetic: none -> 6.57 us  [residuals(): return (doubled, doubled.transpose(1, 0, 2))]
    concatenate x0 -> x1, local copies, waits for them, and re-layouts: none -> 4.4 us  [residuals(): doubled = jnp.concatenate([lane_order, lane_order], axis=-1)]
  transfers between devices with their start and end apart: 5 -> 5, of which waited for: 4 -> 4; matrix products, arithmetic and copies ran while one was open for 20% -> 8% of each run, Pallas kernels for 0% -> 0%
where the time goes in v1:
time: 303 us; the launch traced here: 302 us
  Pallas kernels  137 us (45%)
  waiting for transfers between devices  106 us (35%)
  local copies, waits for them, and re-layouts  21.7 us (7%)
  between operations  13.3 us (4%)
  starting transfers between devices  11.9 us (4%)
  other arithmetic  11.3 us (4%)
    pallas_call x1, Pallas kernels, block_gradients(): pl.pallas_call(functools.partial(gradient_kernel, width), grid=(first //...  137 us
    all_gather x1, waiting for transfers between devices, shards(): every_gain = lax.all_gather(gains, ('row', 'col'), axis=0, tiled=True)  51 us
    reduce_scatter x1, waiting for transfers between devices, shards(): row_sum = lax.psum_scatter(row_side, 'col', scatter_dimension=0, tiled=True)  26.3 us
    reduce_scatter x1, waiting for transfers between devices, shards(): col_sum = lax.psum_scatter(col_side, 'row', scatter_dimension=0, tiled=True)  20 us
    all_to_all x1, waiting for transfers between devices, shards(): lax.all_to_all(back_col, ('row', 'col'), split_axis=0, concat_axis=0, til...  7.03 us
    transpose x1, other arithmetic, residuals(): return (doubled, doubled.transpose(1, 0, 2))  6.57 us
    all_to_all x1, starting transfers between devices, shards(): lax.all_to_all(back_row, ('row', 'col'), split_axis=0, concat_axis=0, til...  6.49 us
  transfers between devices with their start and end apart: 5, of which 4 were waited for; matrix products, arithmetic and copies ran while one was open for 8% of the time, Pallas kernels for 0%

profile of v1, /device:TPU:1, one launch (start us, length us, event | category | flops | bytes accessed | tf_op | source)
XLA Modules:
  0.0 302.3 jit_solution(3651593718187275626)
XLA Ops:
  6.5 0.7 all-gather.2.cloned.1.call-update
  7.3 0.8 convert_element_type.15
  8.1 1.5 fusion
  9.6 2.7 copy.13
  12.4 6.6 %fusion.14 = (f32[64,128,128]{2,1,0:T(8,128)}, f32[128,64,128]{2,0,1:T(8,128)S(1)}) fusion(f32[128,64,64]{2,0,1:T(8,128)} %copy.13), kind=kLoop, calls=%fused_computation.61 | loop fusion | flops 1048576 | bytes 10485760 | tf_op jit(solution)/shard_map/transpose | solution.py:194
  19.0 4.4 %copy.15.g_ref = f32[128,64,128]{2,1,0:T(8,128)} copy(f32[128,64,128]{2,0,1:T(8,128)S(1)} %get-tuple-element.17) | data formatting | bytes 8388608 | tf_op jit(solution)/shard_map/concatenate | solution.py:193
  23.4 0.1 compare_and_fusion.1
  23.5 51.0 %all-gather.2.cloned.1.call-done = f32[512,8,256]{2,1,0:T(8,128)} async-done(((f32[16,8,256]{2,1,0:T(8,128)}), f32[512,8,256]{2,1,0:T(8,128)}) %all-gather.2.cloned.1.call-update) | async-done | bytes 4194320 | tf_op jit(solution)/shard_map/all_gather | solution.py:273
  74.5 2.8 gather_fusion
  77.4 1.3 broadcast_select_fusion.jr_ref
  78.6 2.8 gather_fusion.1
  81.4 0.9 broadcast_select_fusion.1.jc_ref
  82.3 137.0 %shard_map.55 = (f32[128,8,256]{2,1,0:T(8,128)}, f32[64,8,256]{2,1,0:T(8,128)}) custom-call(bf16[128,64,8,256]{3,2,1,0:T(8,128)(2,1)} %bitcast.29, f32[128,64,128]{2,1,0:T(8,128)} %copy.15.g_ref, f32[64,128,128]{2,1,0:T(8,128)} %get-tuple-element.16.gt_ref, f32[128,8,256]{2,1,0:T(8,128)} %broadcast_select_fusion.jr_ref, ...), custom_call_target="tpu_custom_call" | custom-call | tf_op jit(solution)/shard_map/pallas_call | solution.py:206
  219.4 0.7 reduce-scatter.5.cloned.1.call-update
  220.1 0.7 gather_fusion.3
  220.8 26.3 %reduce-scatter.3.cloned.1.call-done = f32[16,8,256]{2,1,0:T(8,128)} async-done(((f32[128,8,256]{2,1,0:T(8,128)}), f32[16,8,256]{2,1,0:T(8,128)}) %reduce-scatter.3.cloned.1.call-update) | async-done | bytes 131088 | tf_op jit(solution)/shard_map/reduce_scatter | solution.py:279
  247.1 0.9 copy.20
  248.1 0.4 convolution_bitcast_fusion.1
  248.4 1.0 copy.16
  249.4 6.5 %all-to-all-start = ((f32[32,1,2048]{2,1,0:T(1,128)}), f32[32,1,2048]{2,1,0:T(1,128)S(1)}, u32[]{:S(2)}, u32[]{:S(2)}) async-start(f32[32,1,2048]{2,1,0:T(1,128)} %copy.16), calls=%async_computation.1 | async-start | bytes 524288 | tf_op jit(solution)/shard_map/all_to_all | solution.py:284
  255.9 0.7 gather_fusion.4
  256.6 20.0 %reduce-scatter.5.cloned.1.call-done = f32[16,8,256]{2,1,0:T(8,128)} async-done(((f32[64,8,256]{2,1,0:T(8,128)}), f32[16,8,256]{2,1,0:T(8,128)}) %reduce-scatter.5.cloned.1.call-update) | async-done | bytes 131088 | tf_op jit(solution)/shard_map/reduce_scatter | solution.py:280
  276.6 0.9 copy.21
  277.5 0.4 convolution_bitcast_fusion
  277.9 1.0 copy.17
  278.9 5.4 %all-to-all-start.1 = ((f32[32,1,2048]{2,1,0:T(1,128)}), f32[32,1,2048]{2,1,0:T(1,128)S(1)}, u32[]{:S(2)}, u32[]{:S(2)}) async-start(f32[32,1,2048]{2,1,0:T(1,128)} %copy.17), calls=%async_computation.3 | async-start | bytes 524288 | tf_op jit(solution)/shard_map/all_to_all | solution.py:285
  284.3 2.4 scatter_custom_fusion
  286.7 0.7 gather_fusion.2
  287.4 0.3 fusion.3
  287.7 7.0 %all-to-all-done.1 = f32[32,1,2048]{2,1,0:T(1,128)S(1)} async-done(((f32[32,1,2048]{2,1,0:T(1,128)}), f32[32,1,2048]{2,1,0:T(1,128)S(1)}, u32[]{:S(2)}, u32[]{:S(2)}) %all-to-all-start.1) | async-done | bytes 262176 | tf_op jit(solution)/shard_map/all_to_all | solution.py:285
  294.8 0.3 convolution_add_fusion
  295.1 0.7 copy.22
  (19 shorter events, 0.3 us)
Async XLA Ops:
  6.5 68.0 %all-gather.2.cloned.1.call-start = ((), (), s32[]{:S(2)}) async-start(), calls=%async_computation.4 | async-start | bytes 4325376 | tf_op jit(solution)/shard_map/all_gather | solution.py:273
  7.3 239.8 %reduce-scatter.3.cloned.1.call-start = ((), (), s32[]{:S(2)}) async-start(), calls=%async_computation.5 | async-start | bytes 1179648 | tf_op jit(solution)/shard_map/reduce_scatter | solution.py:279
  19.0 4.4 %copy-start = (s32[512]{0:T(512)S(1)}, s32[512]{0:T(512)}, u32[]{:S(2)}) copy-start(s32[512]{0:T(512)} %param.11) | copy-start | bytes 6148
  219.3 57.3 %reduce-scatter.5.cloned.1.call-start = ((), (), s32[]{:S(2)}) async-start(), calls=%async_computation.6 | async-start | bytes 655360 | tf_op jit(solution)/shard_map/reduce_scatter | solution.py:280
  249.4 29.5 %all-to-all-start = ((f32[32,1,2048]{2,1,0:T(1,128)}), f32[32,1,2048]{2,1,0:T(1,128)S(1)}, u32[]{:S(2)}, u32[]{:S(2)}) async-start(f32[32,1,2048]{2,1,0:T(1,128)} %copy.16), calls=%async_computation.1 | async-start | bytes 524288 | tf_op jit(solution)/shard_map/all_to_all | solution.py:284
  278.9 15.9 %all-to-all-start.1 = ((f32[32,1,2048]{2,1,0:T(1,128)}), f32[32,1,2048]{2,1,0:T(1,128)S(1)}, u32[]{:S(2)}, u32[]{:S(2)}) async-start(f32[32,1,2048]{2,1,0:T(1,128)} %copy.17), calls=%async_computation.3 | async-start | bytes 524288 | tf_op jit(solution)/shard_map/all_to_all | solution.py:285
Sparse Core Ops, SparseCore 0:
  10.3 64.1 all-gather.1
  219.4 27.6 reduce-scatter.2
  249.9 26.6 reduce-scatter.4

commit v2 on v1

--- a/solution.py
+++ b/solution.py
@@ -235,20 +235,208 @@
     )(model, doubled, across, row_gains, col_gains)
 
 
-def selector(identifiers, count):
-    return (identifiers[:, None] == jnp.arange(count, dtype=jnp.int32)[None, :]).astype(jnp.float32)
-
-
-def select_rows(table, values):
-    return jnp.dot(
-        table, values, precision=lax.Precision.HIGHEST, preferred_element_type=jnp.float32
+MESH = pl.DeviceIdType.MESH
+
+
+def device(place, col_total):
+    return (place // col_total, place % col_total)
+
+
+def remote(source, target, send_sem, recv_sem, where):
+    return pltpu.make_async_remote_copy(
+        src_ref=source,
+        dst_ref=target,
+        send_sem=send_sem,
+        recv_sem=recv_sem,
+        device_id=where,
+        device_id_type=MESH,
     )
+
+
+def each(start, stop, action):
+    def body(index, carry):
+        action(index)
+        return carry
+
+    lax.fori_loop(start, stop, body, 0)
+
+
+def greet(me, total, col_total):
+    barrier = pltpu.get_barrier_semaphore()
+
+    def hello(offset):
+        pl.semaphore_signal(
+            barrier,
+            inc=1,
+            device_id=device(lax.rem(me + offset, total), col_total),
+            device_id_type=MESH,
+        )
+
+    each(1, total, hello)
+    pl.semaphore_wait(barrier, total - 1)
+
+
+def exchange(send_ref, recv_ref, send_sems, recv_sems, me, total, col_total):
+    def copy(offset):
+        place = lax.rem(me + offset, total)
+        return remote(
+            send_ref.at[place],
+            recv_ref.at[me],
+            send_sems.at[offset],
+            recv_sems.at[offset],
+            device(place, col_total),
+        )
+
+    each(1, total, lambda offset: copy(offset).start())
+    recv_ref[me] = send_ref[me]
+    each(1, total, lambda offset: copy(offset).wait())
+
+
+def spread_kernel(
+    row_total, col_total, holders_ref, send_ref, row_ref, col_ref,
+    recv_ref, x_send, x_recv, c_send, c_recv, a_send, a_recv, b_send, b_recv,
+):
+    share = holders_ref.shape[1]
+    r = lax.axis_index("row")
+    c = lax.axis_index("col")
+    total = row_total * col_total
+    me = r * col_total + c
+    greet(me, total, col_total)
+    exchange(send_ref, recv_ref, x_send, x_recv, me, total, col_total)
+
+    def choose(j):
+        row_ref[c * share + j] = recv_ref[holders_ref[0, j], 0]
+        col_ref[r * share + j] = recv_ref[holders_ref[1, j], 1]
+
+    each(0, share, choose)
+    half = col_total // 2
+    partner = c + 1 - 2 * (c % 2)
+
+    def col_copy(offset):
+        block = col_ref.at[pl.ds(r * share, share)]
+        where = (lax.rem(r + offset, row_total), c)
+        return remote(block, block, c_send.at[offset], c_recv.at[offset], where)
+
+    def far_copy(offset):
+        block = row_ref.at[pl.ds(c * share, share)]
+        where = (r, lax.rem(c + 2 * offset, col_total))
+        return remote(block, block, a_send.at[offset], a_recv.at[offset], where)
+
+    def near_copy(offset):
+        origin = lax.rem(c + col_total - 2 * offset, col_total)
+        block = row_ref.at[pl.ds(origin * share, share)]
+        return remote(block, block, b_send.at[offset], b_recv.at[offset], (r, partner))
+
+    each(1, half, lambda offset: far_copy(offset).start())
+    each(1, row_total, lambda offset: col_copy(offset).start())
+    near_copy(0).start()
+
+    def forward(offset):
+        far_copy(offset).wait_recv()
+        near_copy(offset).start()
+
+    each(1, half, forward)
+    each(1, half, lambda offset: far_copy(offset).wait_send())
+    each(0, half, lambda offset: near_copy(offset).wait())
+    each(1, row_total, lambda offset: col_copy(offset).wait())
+
+
+def collect_kernel(
+    row_total, col_total, back_ref, own_ref, row_ref, col_ref, out_ref,
+    pair_ref, part_ref, far_ref, colin_ref, sums_ref, send_ref, recv_ref,
+    x_send, x_recv, c_send, c_recv, a_send, a_recv, b_send, b_recv,
+):
+    share = own_ref.shape[1]
+    r = lax.axis_index("row")
+    c = lax.axis_index("col")
+    total = row_total * col_total
+    me = r * col_total + c
+    half = col_total // 2
+    core = c % 2
+    chip = c // 2
+    greet(me, total, col_total)
+
+    def near_copy(offset):
+        q = lax.rem(chip + offset, half)
+        block = row_ref.at[pl.ds((2 * q + 1 - core) * share, share)]
+        return remote(
+            block, pair_ref.at[q], a_send.at[offset], a_recv.at[offset], (r, 2 * chip + 1 - core)
+        )
+
+    def far_copy(offset):
+        q = lax.rem(chip + offset, half)
+        return remote(
+            part_ref.at[q], far_ref.at[offset], b_send.at[offset], b_recv.at[offset],
+            (r, 2 * q + core),
+        )
+
+    def col_copy(offset):
+        there = lax.rem(r + offset, row_total)
+        block = col_ref.at[pl.ds(there * share, share)]
+        return remote(
+            block, colin_ref.at[offset], c_send.at[offset], c_recv.at[offset], (there, c)
+        )
+
+    def join(offset):
+        near_copy(offset).wait_recv()
+        q = lax.rem(chip + offset, half)
+        part_ref[q] = row_ref[pl.ds((2 * q + core) * share, share)] + pair_ref[q]
+
+    def join_and_send(offset):
+        join(offset)
+        far_copy(offset).start()
+
+    each(1, half + 1, lambda offset: near_copy(lax.rem(offset, half)).start())
+    each(1, row_total, lambda offset: col_copy(offset).start())
+    each(1, half, join_and_send)
+    join(0)
+    sums_ref[0] = part_ref[chip]
+    sums_ref[1] = col_ref[pl.ds(r * share, share)]
+
+    def add_col(offset):
+        col_copy(offset).wait()
+        sums_ref[1] += colin_ref[offset]
+
+    def add_row(offset):
+        far_copy(offset).wait()
+        sums_ref[0] += far_ref[offset]
+
+    each(1, row_total, add_col)
+    each(1, half, add_row)
+    each(0, half, lambda offset: near_copy(offset).wait_send())
+
+    def address(place):
+        send_ref[place, 0] = sums_ref[0, back_ref[0, place]]
+        send_ref[place, 1] = sums_ref[1, back_ref[1, place]]
+
+    each(0, total, address)
+    exchange(send_ref, recv_ref, x_send, x_recv, me, total, col_total)
+
+    def settle(j):
+        out_ref[j] = recv_ref[own_ref[0, j], 0] + recv_ref[own_ref[1, j], 1]
+
+    each(0, share, settle)
+
+
+def semaphores(total, row_total, col_total):
+    counts = (total, row_total, col_total // 2, col_total // 2)
+    return [pltpu.SemaphoreType.DMA((count,)) for count in counts for _ in range(2)]
+
+
+def places(identifiers, count):
+    here = identifiers[:, None] == jnp.arange(count, dtype=jnp.int32)[None, :]
+    index = jnp.arange(identifiers.shape[0], dtype=jnp.int32)[:, None]
+    return jnp.sum(jnp.where(here, index, 0), axis=0, dtype=jnp.int32)
+
+
+def call_options(identifier):
+    return pltpu.CompilerParams(collective_id=identifier, has_side_effects=True)
 
 
 def shards(gains, coherency, cotangent, flags, station_slot):
     stations = station_slot.shape[0]
     share = gains.shape[0]
-    flat = gains.shape[1] * gains.shape[2]
+    tail = gains.shape[1:]
     row_total = lax.axis_size("row")
     col_total = lax.axis_size("col")
     groups = row_total * col_total
@@ -256,38 +444,55 @@
     col_place = lax.axis_index("col")
     device_place = row_place * col_total + col_place
     counting = jnp.arange(share, dtype=jnp.int32)
-    slot_of = (
-        jnp.zeros((stations,), jnp.int32)
-        .at[station_slot]
-        .set(jnp.arange(stations, dtype=jnp.int32))
-    )
-    own_blocks = jnp.take(slot_of, device_place * share + counting) // share
+    mine = device_place * share + counting
+    found = station_slot[None, :] == mine[:, None]
+    slot_index = jnp.arange(stations, dtype=jnp.int32)[None, :]
+    own_blocks = jnp.sum(jnp.where(found, slot_index, 0), axis=1, dtype=jnp.int32) // share
     col_target = own_blocks % row_total * col_total + own_blocks // row_total
     col_block = col_place * row_total + row_place
-    row_holder = jnp.take(station_slot, device_place * share + counting) // share
-    col_holder = jnp.take(station_slot, col_block * share + counting) // share
-    row_count = coherency.shape[0]
-    col_count = coherency.shape[1]
-    row_ids = lax.dynamic_slice_in_dim(station_slot, row_place * row_count, row_count)
-    col_ids = lax.dynamic_slice_in_dim(station_slot, col_place * col_count, col_count)
-    every_gain = lax.all_gather(gains, ("row", "col"), axis=0, tiled=True)
-    row_gains = jnp.take(every_gain, row_ids, axis=0)
-    col_gains = jnp.take(every_gain, col_ids, axis=0)
+    row_holder = lax.dynamic_slice_in_dim(station_slot, device_place * share, share) // share
+    col_holder = lax.dynamic_slice_in_dim(station_slot, col_block * share, share) // share
+    holders = jnp.stack([row_holder, col_holder])
+    targets = jnp.stack([own_blocks, col_target])
+    picks = jnp.stack([places(own_blocks, groups), places(col_target, groups)], axis=1)
+    sent = jnp.take(gains, picks.reshape(-1), axis=0).reshape((groups, 2) + tail)
+    vmem = pl.BlockSpec(memory_space=pltpu.VMEM)
+    smem = pl.BlockSpec(memory_space=pltpu.SMEM)
+    f32 = jnp.float32
+    table = pltpu.VMEM((groups, 2) + tail, f32)
+    row_gains, col_gains = pl.pallas_call(
+        functools.partial(spread_kernel, row_total, col_total),
+        in_specs=[smem, vmem],
+        out_specs=[vmem, vmem],
+        out_shape=[
+            jax.ShapeDtypeStruct((col_total * share,) + tail, f32),
+            jax.ShapeDtypeStruct((row_total * share,) + tail, f32),
+        ],
+        scratch_shapes=[table] + semaphores(groups, row_total, col_total),
+        compiler_params=call_options(1),
+    )(holders, sent)
     row_side, col_side = block_gradients(
         coherency, *residuals(cotangent, flags), row_gains, col_gains
     )
-    row_sum = lax.psum_scatter(row_side, "col", scatter_dimension=0, tiled=True)
-    col_sum = lax.psum_scatter(col_side, "row", scatter_dimension=0, tiled=True)
-    back_row = select_rows(selector(row_holder, groups).T, row_sum.reshape(share, flat))
-    back_col = select_rows(selector(col_holder, groups).T, col_sum.reshape(share, flat))
-    recv_row, recv_col = (
-        lax.all_to_all(back_row, ("row", "col"), split_axis=0, concat_axis=0, tiled=True),
-        lax.all_to_all(back_col, ("row", "col"), split_axis=0, concat_axis=0, tiled=True),
-    )
-    result = select_rows(selector(own_blocks, groups), recv_row) + select_rows(
-        selector(col_target, groups), recv_col
-    )
-    return result.reshape(gains.shape)
+    backs = jnp.stack([places(row_holder, groups), places(col_holder, groups)])
+    half = col_total // 2
+    return pl.pallas_call(
+        functools.partial(collect_kernel, row_total, col_total),
+        in_specs=[smem, smem, vmem, vmem],
+        out_specs=vmem,
+        out_shape=jax.ShapeDtypeStruct(gains.shape, f32),
+        scratch_shapes=[
+            pltpu.VMEM((half, share) + tail, f32),
+            pltpu.VMEM((half, share) + tail, f32),
+            pltpu.VMEM((half, share) + tail, f32),
+            pltpu.VMEM((row_total, share) + tail, f32),
+            pltpu.VMEM((2, share) + tail, f32),
+            table,
+            table,
+        ]
+        + semaphores(groups, row_total, col_total),
+        compiler_params=call_options(2),
+    )(backs, targets, row_side, col_side)
 
 
 def solution(mesh):

time: 303 us -> 226 us (0.75)
  waiting for transfers between devices: 106 us -> 0 us
  Pallas kernels: 137 us -> 202 us
  between operations: 13.3 us -> 0.08 us
  local copies, waits for them, and re-layouts: 21.7 us -> 9.64 us
  starting transfers between devices: 11.9 us -> 0 us
    pallas_call x0 -> x2, Pallas kernels: none -> 68.8 us  [the longest x1 35.4 us: shards(): pl.pallas_call(functools.partial(spread_kernel, row_total, col_total), in...]
    all_gather x1 -> x0, waiting for transfers between devices: 51 us -> none  [shards(): every_gain = lax.all_gather(gains, ('row', 'col'), axis=0, tiled=True)]
    reduce_scatter x2 -> x0, waiting for transfers between devices: 46.3 us -> none  [the longest x1 26.3 us: shards(): row_sum = lax.psum_scatter(row_side, 'col', scatter_dimension=0, tiled=True)]
    all_to_all x2 -> x0, starting transfers between devices: 11.9 us -> none  [the longest x1 6.49 us: shards(): lax.all_to_all(back_row, ('row', 'col'), split_axis=0, concat_axis=0, til...]
    all_to_all x2 -> x0, waiting for transfers between devices: 7.04 us -> none  [the longest x1 7.03 us: shards(): lax.all_to_all(back_col, ('row', 'col'), split_axis=0, concat_axis=0, til...]
    gather x5 -> x1, local copies, waits for them, and re-layouts: 7.61 us -> 0.63 us  [shards(): jnp.take(gains, picks.reshape(-1), axis=0).reshape((groups, 2) + tail)]
    pallas_call x1, Pallas kernels: 137 us -> 133 us  [block_gradients(): pl.pallas_call(functools.partial(gradient_kernel, width), grid=(first //...]
  transfers between devices with their start and end apart: 5 -> 0, of which waited for: 4 -> 0; matrix products, arithmetic and copies ran while one was open for 8% -> 0% of each run, Pallas kernels for 0% -> 0%
where the time goes in v2:
time: 226 us; the launch traced here: 225 us
  Pallas kernels  202 us (89%)
  other arithmetic  13.4 us (6%)
  local copies, waits for them, and re-layouts  9.64 us (4%)
    pallas_call x1, Pallas kernels, block_gradients(): pl.pallas_call(functools.partial(gradient_kernel, width), grid=(first //...  133 us
    pallas_call x1, Pallas kernels, shards(): pl.pallas_call(functools.partial(spread_kernel, row_total, col_total), in...  35.4 us
    pallas_call x1, Pallas kernels, shards(): pl.pallas_call(functools.partial(collect_kernel, row_total, col_total), i...  33.4 us
    transpose x1, other arithmetic, residuals(): return (doubled, doubled.transpose(1, 0, 2))  6.54 us

profile of v2, /device:TPU:1, one launch (start us, length us, event | category | flops | bytes accessed | tf_op | source)
XLA Modules:
  0.0 225.0 jit_solution(10925169641176689568)
XLA Ops:
  0.0 0.0 copy-start
  0.0 0.8 and_select_fusion.7
  0.8 0.1 select_reduce_fusion.3
  0.9 0.6 pad_add_fusion.back_ref
  1.5 0.9 select_reduce_fusion
  2.4 0.6 pad_add_fusion.1.own_ref
  3.0 0.8 convert_element_type.11
  3.7 1.5 fusion
  5.3 2.7 %copy.17 = f32[128,64,64]{2,0,1:T(8,128)} copy(f32[128,64,64]{0,2,1:T(8,128)S(1)} %fusion) | data formatting | bytes 4194304 | tf_op jit(solution)/shard_map/reshape | solution.py:192
  8.0 6.5 %fusion.6 = (f32[64,128,128]{2,1,0:T(8,128)}, f32[128,64,128]{2,0,1:T(8,128)S(1)}) fusion(f32[128,64,64]{2,0,1:T(8,128)} %copy.17), kind=kLoop, calls=%fused_computation.55 | loop fusion | flops 1048576 | bytes 10485760 | tf_op jit(solution)/shard_map/transpose | solution.py:194
  14.6 4.4 %copy.21.g_ref = f32[128,64,128]{2,1,0:T(8,128)} copy(f32[128,64,128]{2,0,1:T(8,128)S(1)} %get-tuple-element.16) | data formatting | bytes 8388608 | tf_op jit(solution)/shard_map/concatenate | solution.py:193
  19.0 0.5 pad_add_fusion.2.holders_ref
  19.5 0.1 select_reduce_fusion.1
  19.6 0.1 copy.20
  19.7 0.1 reshape.228
  19.8 0.0 copy-done
  19.8 0.6 gather_fusion
  20.5 0.1 copy.19
  20.6 0.9 broadcast_select_fusion.send_ref
  21.5 35.4 %shard_map.55 = (f32[128,8,256]{2,1,0:T(8,128)}, f32[64,8,256]{2,1,0:T(8,128)}) custom-call(s32[2,16]{1,0:T(2,128)} %pad_add_fusion.2.holders_ref, f32[32,2,8,256]{3,2,1,0:T(8,128)} %broadcast_select_fusion.send_ref), custom_call_target="tpu_custom_call" | custom-call | tf_op jit(solution)/shard_map/pallas_call | solution.py:463
  56.9 133.1 %shard_map.56 = (f32[128,8,256]{2,1,0:T(8,128)}, f32[64,8,256]{2,1,0:T(8,128)}) custom-call(bf16[128,64,8,256]{3,2,1,0:T(8,128)(2,1)} %bitcast.30, f32[128,64,128]{2,1,0:T(8,128)} %copy.21.g_ref, f32[64,128,128]{2,1,0:T(8,128)} %get-tuple-element.15.gt_ref, f32[128,8,256]{2,1,0:T(8,128)} %get-tuple-element.9.jr_ref, f32[64,8,256]{2,1,0:T(8,128)} %get-tuple-element.10.jc_ref), custom_call_target="tpu_custom_call" | custom-call | tf_op jit(solution)/shard_map/pallas_call | solution.py:206
  190.1 33.4 %shard_map.57 = f32[16,8,256]{2,1,0:T(8,128)} custom-call(s32[2,32]{1,0:T(2,128)} %pad_add_fusion.back_ref, s32[2,16]{1,0:T(2,128)} %pad_add_fusion.1.own_ref, f32[128,8,256]{2,1,0:T(8,128)} %get-tuple-element.11.row_ref, f32[64,8,256]{2,1,0:T(8,128)} %get-tuple-element.12.col_ref), custom_call_target="tpu_custom_call" | custom-call | tf_op jit(solution)/shard_map/pallas_call | solution.py:479
  223.5 1.6 copy.24
  (7 shorter events, 0.1 us)
Async XLA Ops:
  0.0 19.8 %copy-start = (f32[16,8,256]{2,1,0:T(8,128)S(1)}, f32[16,8,256]{2,1,0:T(8,128)}, u32[]{:S(2)}) copy-start(f32[16,8,256]{2,1,0:T(8,128)} %param.5) | copy-start | bytes 393220

commit v3 on v2

--- a/solution.py
+++ b/solution.py
@@ -60,12 +60,12 @@
 
 
 def gradient_kernel(
-    width, m_ref, g_ref, gt_ref, jr_ref, jc_ref, r_ref, c_ref,
+    width, m_ref, gt_ref, jr_ref, jc_ref, r_ref, c_ref,
     wr_ref, wc_ref, xr_ref, xa_ref, xb_ref, acc_ref,
 ):
     block, second, channels, _ = m_ref.shape
     lanes = 4 * width
-    depth = g_ref.shape[2]
+    depth = gt_ref.shape[2]
     pair = xa_ref.shape[0]
     chunk = xa_ref.shape[1] // channels
     chunks = second // chunk
@@ -90,12 +90,12 @@
 
     def spread(rows):
         count = rows.shape[0]
-        wide = rows[:, None, :] * diagonal[None]
+        wide = rows * diagonal[None]
         return wide.reshape(count * channels, depth).astype(jnp.bfloat16)
 
     def row_products(k, carry):
         xr_ref[k] = jnp.dot(
-            spread(gt_ref[k]), wr_ref[k], preferred_element_type=jnp.float32
+            spread(gt_ref[k][:, None, :]), wr_ref[k], preferred_element_type=jnp.float32
         )
         return carry
 
@@ -110,7 +110,7 @@
             start = pl.multiple_of(at * chunk, chunk)
             for p in range(pair):
                 x_ref[p] = jnp.dot(
-                    spread(g_ref[first + p, pl.ds(start, chunk)]),
+                    spread(gt_ref[pl.ds(start, chunk), pl.ds(first + p, 1)]),
                     wc_ref[p],
                     preferred_element_type=jnp.float32,
                 )
@@ -189,18 +189,17 @@
 def residuals(cotangent, flags):
     first, second, channels = cotangent.shape[:3]
     weighted = cotangent[:, :, :, 0].astype(jnp.float32) * flags.astype(jnp.float32)[..., None]
-    lane_order = weighted.transpose(0, 1, 3, 2).reshape(first, second, 8 * channels)
-    doubled = jnp.concatenate([lane_order, lane_order], axis=-1)
-    return doubled, doubled.transpose(1, 0, 2)
-
-
-def block_gradients(coherency, doubled, across, row_gains, col_gains):
+    lane_order = weighted.transpose(1, 0, 3, 2).reshape(second, first, 8 * channels)
+    return jnp.concatenate([lane_order, lane_order], axis=-1)
+
+
+def block_gradients(coherency, across, row_gains, col_gains):
     first, second, channels, _, wide = coherency.shape
     width = wide // 8
-    block = min(16, first)
+    block = min(32, first)
     pair = 2
     chunk = min(16, second // 2)
-    depth = doubled.shape[2]
+    depth = across.shape[2]
     model = coherency.reshape(first, second, channels, wide)
     products = (pair, chunk * channels, 2 * wide)
     return pl.pallas_call(
@@ -208,7 +207,6 @@
         grid=(first // block,),
         in_specs=[
             pl.BlockSpec((block, second, channels, wide), lambda s: (s, 0, 0, 0)),
-            pl.BlockSpec((block, second, depth), lambda s: (s, 0, 0)),
             pl.BlockSpec((second, block, depth), lambda s: (0, s, 0)),
             pl.BlockSpec((block, channels, wide), lambda s: (s, 0, 0)),
             pl.BlockSpec((second, channels, wide), lambda s: (0, 0, 0)),
@@ -232,7 +230,7 @@
         compiler_params=pltpu.CompilerParams(
             dimension_semantics=("arbitrary",), vmem_limit_bytes=58 * 1024 * 1024
         ),
-    )(model, doubled, across, row_gains, col_gains)
+    )(model, across, row_gains, col_gains)
 
 
 MESH = pl.DeviceIdType.MESH
@@ -472,7 +470,7 @@
         compiler_params=call_options(1),
     )(holders, sent)
     row_side, col_side = block_gradients(
-        coherency, *residuals(cotangent, flags), row_gains, col_gains
+        coherency, residuals(cotangent, flags), row_gains, col_gains
     )
     backs = jnp.stack([places(row_holder, groups), places(col_holder, groups)])
     half = col_total // 2

time: 226 us -> 212 us (0.938)
  Pallas kernels: 202 us -> 192 us
  local copies, waits for them, and re-layouts: 9.64 us -> 5.24 us
    pallas_call x1, Pallas kernels: 133 us -> 123 us  [block_gradients(): pl.pallas_call(functools.partial(gradient_kernel, width), grid=(first //...]
    transpose x1 -> x0, other arithmetic: 6.54 us -> none  [residuals(): return (doubled, doubled.transpose(1, 0, 2))]
    concatenate x0 -> x1, other arithmetic: none -> 6.54 us  [residuals(): return jnp.concatenate([lane_order, lane_order], axis=-1)]
    concatenate x1 -> x0, local copies, waits for them, and re-layouts: 4.4 us -> none  [residuals(): doubled = jnp.concatenate([lane_order, lane_order], axis=-1)]
where the time goes in v3:
time: 212 us; the launch traced here: 211 us
  Pallas kernels  192 us (91%)
  other arithmetic  13.5 us (6%)
  local copies, waits for them, and re-layouts  5.24 us (2%)
    pallas_call x1, Pallas kernels, block_gradients(): pl.pallas_call(functools.partial(gradient_kernel, width), grid=(first //...  123 us
    pallas_call x1, Pallas kernels, shards(): pl.pallas_call(functools.partial(spread_kernel, row_total, col_total), in...  35.3 us
    pallas_call x1, Pallas kernels, shards(): pl.pallas_call(functools.partial(collect_kernel, row_total, col_total), i...  33.4 us
    concatenate x1, other arithmetic, residuals(): return jnp.concatenate([lane_order, lane_order], axis=-1)  6.54 us

profile of v3, /device:TPU:1, one launch (start us, length us, event | category | flops | bytes accessed | tf_op | source)
XLA Modules:
  0.0 210.8 jit_solution(16846646598862149445)
XLA Ops:
  0.0 0.0 copy-start
  0.0 0.8 and_select_fusion.7
  0.8 0.1 select_reduce_fusion.3
  0.9 0.6 pad_add_fusion.back_ref
  1.5 0.9 select_reduce_fusion
  2.4 0.5 pad_add_fusion.1.own_ref
  2.9 0.8 convert_element_type.11
  3.7 1.5 fusion
  5.3 2.7 %copy.15 = f32[64,128,64]{2,1,0:T(8,128)} copy(f32[64,128,64]{1,2,0:T(8,128)S(1)} %fusion) | data formatting | bytes 4194304 | tf_op jit(solution)/shard_map/reshape | solution.py:192
  8.0 6.5 %pad_maximum_fusion.gt_ref = f32[64,128,128]{2,1,0:T(8,128)} fusion(f32[64,128,64]{2,1,0:T(8,128)} %copy.15), kind=kLoop, calls=%fused_computation.1 | loop fusion | flops 1048576 | bytes 6291456 | tf_op jit(solution)/shard_map/concatenate | solution.py:193
  14.6 0.6 pad_add_fusion.2.holders_ref
  15.2 0.1 select_reduce_fusion.1
  15.3 0.1 copy.18
  15.4 0.1 reshape.228
  15.5 0.0 copy-done
  15.5 0.6 gather_fusion
  16.2 0.1 copy.17
  16.3 0.9 broadcast_select_fusion.send_ref
  17.2 35.3 %shard_map.55 = (f32[128,8,256]{2,1,0:T(8,128)}, f32[64,8,256]{2,1,0:T(8,128)}) custom-call(s32[2,16]{1,0:T(2,128)} %pad_add_fusion.2.holders_ref, f32[32,2,8,256]{3,2,1,0:T(8,128)} %broadcast_select_fusion.send_ref), custom_call_target="tpu_custom_call" | custom-call | tf_op jit(solution)/shard_map/pallas_call | solution.py:461
  52.6 123.3 %shard_map.56 = (f32[128,8,256]{2,1,0:T(8,128)}, f32[64,8,256]{2,1,0:T(8,128)}) custom-call(bf16[128,64,8,256]{3,2,1,0:T(8,128)(2,1)} %bitcast.28, f32[64,128,128]{2,1,0:T(8,128)} %pad_maximum_fusion.gt_ref, f32[128,8,256]{2,1,0:T(8,128)} %get-tuple-element.9.jr_ref, f32[64,8,256]{2,1,0:T(8,128)} %get-tuple-element.10.jc_ref), custom_call_target="tpu_custom_call" | custom-call | tf_op jit(solution)/shard_map/pallas_call | solution.py:205
  175.9 33.4 %shard_map.57 = f32[16,8,256]{2,1,0:T(8,128)} custom-call(s32[2,32]{1,0:T(2,128)} %pad_add_fusion.back_ref, s32[2,16]{1,0:T(2,128)} %pad_add_fusion.1.own_ref, f32[128,8,256]{2,1,0:T(8,128)} %get-tuple-element.11.row_ref, f32[64,8,256]{2,1,0:T(8,128)} %get-tuple-element.12.col_ref), custom_call_target="tpu_custom_call" | custom-call | tf_op jit(solution)/shard_map/pallas_call | solution.py:477
  209.3 1.6 copy.21
  (7 shorter events, 0.1 us)
Async XLA Ops:
  0.0 15.5 %copy-start = (f32[16,8,256]{2,1,0:T(8,128)S(1)}, f32[16,8,256]{2,1,0:T(8,128)}, u32[]{:S(2)}) copy-start(f32[16,8,256]{2,1,0:T(8,128)} %param.5) | copy-start | bytes 393220
